TPU v7x, 32 devices: a whole 2x2x4 slice. The times are simulated.
32 devices in a mesh: dp: 4 (over y, x), frame: 2 (over core), tensor: 4 (over z).
Axes of the slice: x: 2, y: 2, z: 4, core: 2. Of those that a mesh axis runs over, the one named last changes fastest.
Arguments:
- tokens: bfloat16 [8, 8, 256, 1024], P('dp', ('frame', 'tensor')), may hold values from -6 to 6
- out_grad: bfloat16 [8, 8, 256, 1024], P('dp', ('frame', 'tensor')), may hold values from -6 to 6
- noise_index: int32 [8, 8], P('dp', 'frame'), may hold values from 0 to 999, as said below
- qkv_weight: bfloat16 [1024, 3, 1024], P(('dp', 'frame'), None, 'tensor'), may hold values from -0.1875 to 0.1875
- out_weight: bfloat16 [1024, 1024], P(('dp', 'frame'), 'tensor'), may hold values from -0.75 to 0.75
- up_weight: bfloat16 [1024, 4096], P(('dp', 'frame'), 'tensor'), may hold values from -0.1875 to 0.1875
- down_weight: bfloat16 [1024, 4096], P(('dp', 'frame'), 'tensor'), may hold values from -0.09375 to 0.09375
- ada_weight: bfloat16 [1024, 6, 1024], P(('dp', 'frame'), None, 'tensor'), may hold values from -0.25 to 0.25
Outputs:
- result: bfloat16 [8, 8, 256, 1024], P('dp', ('frame', 'tensor'))
- input_grad: bfloat16 [8, 8, 256, 1024], P('dp', ('frame', 'tensor'))
- qkv_grad: float32 [1024, 3, 1024], P(('dp', 'frame'), None, 'tensor')
- out_weight_grad: float32 [1024, 1024], P(('dp', 'frame'), 'tensor')
- up_grad: float32 [1024, 4096], P(('dp', 'frame'), 'tensor')
- down_grad: float32 [1024, 4096], P(('dp', 'frame'), 'tensor')
- ada_grad: float32 [1024, 6, 1024], P(('dp', 'frame'), None, 'tensor')
Inputs may be any that keep to these rules, and one draw needn't show every extreme that they name: `noise_index`: each frame's noise level, most often near 1000 - 1.
All inputs are finite; a program needn't handle non-finite values.
Results may differ from a plain program's by a relative error of at most 0.018.
Values may be sent and summed in bfloat16 or wider, within the bound.
A program may use at most 192 MiB of HBM per device.

v0:
```python
import math
import jax
import jax.numpy as jnp
from jax import lax
from jax.sharding import PartitionSpec as P

HEAD_DIM = 64
epsilon = 1e-06
highest = lax.Precision.HIGHEST


def normalize(values):
    center = values - jnp.mean(values, axis=-1, keepdims=True)
    spread = jnp.mean(center * center, axis=-1, keepdims=True)
    inverse = lax.rsqrt(spread + epsilon)
    return (center * inverse, inverse)


def norm_back(upstream, normed, inverse):
    upstream_mean = jnp.mean(upstream, axis=-1, keepdims=True)
    product_mean = jnp.mean(upstream * normed, axis=-1, keepdims=True)
    return inverse * (upstream - upstream_mean - normed * product_mean)


def level_embedding(levels, model_width):
    halfway = model_width // 2
    frequency = jnp.exp(-math.log(10000.0) * jnp.arange(halfway, dtype=jnp.float32) / halfway)
    angles = levels.astype(jnp.float32)[..., None] * frequency
    return jnp.concatenate([jnp.cos(angles), jnp.sin(angles)], axis=-1)


def gelu_tanh(values):
    return jax.nn.gelu(values, approximate=True)


def on_device(
    tokens, out_grad, noise_index, qkv_weight, out_weight, up_weight, down_weight, ada_weight
):
    clips = tokens.shape[0]
    patches = tokens.shape[2]
    model_width = tokens.shape[-1]
    local_width = qkv_weight.shape[2]
    rows_here = qkv_weight.shape[0]
    heads_here = local_width // HEAD_DIM
    scaling = HEAD_DIM ** (-0.5)
    groups = lax.axis_size("tensor")
    halves = lax.axis_size("frame")
    replicas = lax.axis_size("dp")
    with jax.named_scope("modulation"):
        levels_all = lax.all_gather(noise_index, ("dp", "frame"), axis=0, tiled=True)
        levels_all = levels_all.reshape(replicas * halves, clips, groups)
        condition_all = jax.nn.silu(level_embedding(levels_all, model_width)).astype(jnp.bfloat16)
        row_block = lax.axis_index("dp") * halves + lax.axis_index("frame")
        my_condition = lax.dynamic_slice_in_dim(
            condition_all, row_block * rows_here, rows_here, axis=3
        )
        partial_mod = jnp.einsum(
            "acgd,dkw->acgkw", my_condition, ada_weight, preferred_element_type=jnp.float32
        )
        summed_mod = lax.psum_scatter(
            partial_mod, ("dp", "frame"), scatter_dimension=0, tiled=True
        )[0]
        modulation = lax.all_to_all(summed_mod, "tensor", 1, 3, tiled=True)
        modulation = modulation.reshape(clips, 6, 1, model_width)
    with jax.named_scope("weights"):
        joint_weight, mixer_weight, upward_weight, downward_weight = (
            lax.all_gather(w, ("dp", "frame"), axis=0, tiled=True)
            for w in (qkv_weight, out_weight, up_weight, down_weight)
        )
    residual = tokens[:, 0].astype(jnp.float32)
    upstream = out_grad[:, 0].astype(jnp.float32)
    shift1, scale1, gate1 = (modulation[:, 0], modulation[:, 1], modulation[:, 2])
    shift2, scale2, gate2 = (modulation[:, 3], modulation[:, 4], modulation[:, 5])

    def gather_tokens(values):
        return lax.all_gather(values, "tensor", axis=1, tiled=True)

    def scatter_tokens(values):
        return lax.psum_scatter(
            values.astype(jnp.bfloat16), "tensor", scatter_dimension=1, tiled=True
        ).astype(jnp.float32)

    with jax.named_scope("forward"):
        normed_one, inverse_one = normalize(residual)
        entering_one = (normed_one * (1.0 + scale1) + shift1).astype(jnp.bfloat16)
        flat_one = gather_tokens(entering_one)
        token_count = flat_one.shape[1]
        projected = jnp.einsum(
            "crd,dkh->crkh", flat_one, joint_weight, preferred_element_type=jnp.float32
        ).astype(jnp.bfloat16)
        queries = projected[:, :, 0]
        keys_all = lax.all_gather(projected[:, :, 1], "frame", axis=1, tiled=True)
        values_all = lax.all_gather(projected[:, :, 2], "frame", axis=1, tiled=True)
        key_heads = keys_all.reshape(clips, -1, heads_here, HEAD_DIM)
        value_heads = values_all.reshape(clips, -1, heads_here, HEAD_DIM)
        block_rows = min(512, token_count)
        block_count = token_count // block_rows
        query_blocks = jnp.moveaxis(
            queries.reshape(clips, block_count, block_rows, heads_here, HEAD_DIM), 1, 0
        )

        def attend(query_block):
            scores = (
                jnp.einsum(
                    "cqhe,ckhe->chqk", query_block, key_heads, preferred_element_type=jnp.float32
                )
                * scaling
            )
            largest = jnp.max(scores, axis=-1, keepdims=True)
            raised = jnp.exp(scores - largest)
            totals_row = jnp.sum(raised, axis=-1, keepdims=True)
            probs_low = (raised / totals_row).astype(jnp.bfloat16)
            outputs = jnp.einsum(
                "chqk,ckhe->cqhe", probs_low, value_heads, preferred_element_type=jnp.float32
            )
            return (outputs.astype(jnp.bfloat16), (largest + jnp.log(totals_row))[..., 0])

        attended_blocks, log_totals = lax.map(attend, query_blocks)
        attended = jnp.moveaxis(attended_blocks, 0, 1).reshape(clips, token_count, local_width)
        partial_one = jnp.einsum(
            "crh,oh->cro", attended, mixer_weight, preferred_element_type=jnp.float32
        )
        branch_one = scatter_tokens(partial_one)
        middle = residual + gate1 * branch_one
        normed_two, inverse_two = normalize(middle)
        entering_two = (normed_two * (1.0 + scale2) + shift2).astype(jnp.bfloat16)
        flat_two = gather_tokens(entering_two)
        up_values = jnp.einsum(
            "crd,df->crf", flat_two, upward_weight, preferred_element_type=jnp.float32
        )
        hidden = gelu_tanh(up_values).astype(jnp.bfloat16)
        partial_two = jnp.einsum(
            "crf,of->cro", hidden, downward_weight, preferred_element_type=jnp.float32
        )
        branch_two = scatter_tokens(partial_two)
        output = (middle + gate2 * branch_two).astype(jnp.bfloat16)
    with jax.named_scope("backward_ffn"):
        grad_gate_two = jnp.sum(upstream * branch_two, axis=1)
        grad_branch_two = (gate2 * upstream).astype(jnp.bfloat16)
        grad_two_all = gather_tokens(grad_branch_two)
        grad_hidden = jnp.einsum(
            "cro,of->crf", grad_two_all, downward_weight, preferred_element_type=jnp.float32
        )
        down_total = jnp.einsum(
            "cro,crf->of", grad_two_all, hidden, preferred_element_type=jnp.float32
        )
        _, gelu_pullback = jax.vjp(gelu_tanh, up_values)
        grad_up = gelu_pullback(grad_hidden)[0].astype(jnp.bfloat16)
        up_total = jnp.einsum("crd,crf->df", flat_two, grad_up, preferred_element_type=jnp.float32)
        partial_back_two = jnp.einsum(
            "crf,df->crd", grad_up, upward_weight, preferred_element_type=jnp.float32
        )
        grad_entering_two = scatter_tokens(partial_back_two)
        grad_shift_two = jnp.sum(grad_entering_two, axis=1)
        grad_scale_two = jnp.sum(grad_entering_two * normed_two, axis=1)
        grad_middle = upstream + norm_back(
            grad_entering_two * (1.0 + scale2), normed_two, inverse_two
        )
        grad_gate_one = jnp.sum(grad_middle * branch_one, axis=1)
    with jax.named_scope("backward_attention"):
        grad_branch_one = (gate1 * grad_middle).astype(jnp.bfloat16)
        grad_one_all = gather_tokens(grad_branch_one)
        grad_attended = jnp.einsum(
            "cro,oh->crh", grad_one_all, mixer_weight, preferred_element_type=jnp.float32
        ).astype(jnp.bfloat16)
        mixer_total = jnp.einsum(
            "cro,crh->oh", grad_one_all, attended, preferred_element_type=jnp.float32
        )
        grad_blocks = jnp.moveaxis(
            grad_attended.reshape(clips, block_count, block_rows, heads_here, HEAD_DIM), 1, 0
        )

        def attend_back(carried, pieces):
            key_sum, value_sum = carried
            query_block, grad_block, log_block = pieces
            scores = (
                jnp.einsum(
                    "cqhe,ckhe->chqk", query_block, key_heads, preferred_element_type=jnp.float32
                )
                * scaling
            )
            probs = jnp.exp(scores - log_block[..., None])
            grad_probs = jnp.einsum(
                "cqhe,ckhe->chqk", grad_block, value_heads, preferred_element_type=jnp.float32
            )
            value_sum = value_sum + jnp.einsum(
                "chqk,cqhe->ckhe",
                probs.astype(jnp.bfloat16),
                grad_block,
                preferred_element_type=jnp.float32,
            )
            row_terms = jnp.sum(probs * grad_probs, axis=-1, keepdims=True)
            grad_scores = (probs * (grad_probs - row_terms)).astype(jnp.bfloat16)
            grad_queries = (
                jnp.einsum(
                    "chqk,ckhe->cqhe", grad_scores, key_heads, preferred_element_type=jnp.float32
                )
                * scaling
            )
            key_sum = (
                key_sum
                + jnp.einsum(
                    "chqk,cqhe->ckhe", grad_scores, query_block, preferred_element_type=jnp.float32
                )
                * scaling
            )
            return ((key_sum, value_sum), grad_queries)

        zeros_keys = jnp.zeros(key_heads.shape, jnp.float32)
        (key_grads, value_grads), query_grads = lax.scan(
            attend_back, (zeros_keys, zeros_keys), (query_blocks, grad_blocks, log_totals)
        )
        query_grads = jnp.moveaxis(query_grads, 0, 1).reshape(clips, token_count, local_width)
        key_own, value_own = (
            lax.psum_scatter(
                grads.reshape(clips, -1, local_width).astype(jnp.bfloat16),
                "frame",
                scatter_dimension=1,
                tiled=True,
            ).astype(jnp.float32)
            for grads in (key_grads, value_grads)
        )
        grad_projected = jnp.stack([query_grads, key_own, value_own], axis=2).astype(jnp.bfloat16)
        joint_total = jnp.einsum(
            "crd,crkh->dkh", flat_one, grad_projected, preferred_element_type=jnp.float32
        )
        partial_back_one = jnp.einsum(
            "crkh,dkh->crd", grad_projected, joint_weight, preferred_element_type=jnp.float32
        )
        grad_entering_one = scatter_tokens(partial_back_one)
        grad_shift_one = jnp.sum(grad_entering_one, axis=1)
        grad_scale_one = jnp.sum(grad_entering_one * normed_one, axis=1)
        grad_input = grad_middle + norm_back(
            grad_entering_one * (1.0 + scale1), normed_one, inverse_one
        )
    with jax.named_scope("ada_grad"):
        grad_modulation = jnp.stack(
            [
                grad_shift_one,
                grad_scale_one,
                grad_gate_one,
                grad_shift_two,
                grad_scale_two,
                grad_gate_two,
            ],
            axis=1,
        )
        grad_columns = lax.all_to_all(
            grad_modulation.reshape(clips, 1, 6, model_width), "tensor", 3, 1, tiled=True
        )
        grad_all = lax.all_gather(grad_columns, ("dp", "frame"), axis=0, tiled=True)
        grad_all = grad_all.reshape(replicas * halves, clips, groups, 6, local_width)
        adaptive_total = jnp.einsum(
            "acgd,acgkw->dkw", my_condition.astype(jnp.float32), grad_all, precision=highest
        )
    with jax.named_scope("weight_grads"):
        summed = tuple(
            (
                lax.psum_scatter(
                    total.astype(jnp.bfloat16), ("dp", "frame"), scatter_dimension=0, tiled=True
                ).astype(jnp.float32)
                for total in (joint_total, mixer_total, up_total, down_total)
            )
        )
    result = output[:, None]
    input_grad = grad_input.astype(jnp.bfloat16)[:, None]
    return (result, input_grad, summed[0], summed[1], summed[2], summed[3], adaptive_total)


def solution(mesh):
    return jax.shard_map(
        on_device,
        mesh=mesh,
        in_specs=(
            P("dp", ("frame", "tensor"), None, None),
            P("dp", ("frame", "tensor"), None, None),
            P("dp", "frame"),
            P(("dp", "frame"), None, "tensor"),
            P(("dp", "frame"), "tensor"),
            P(("dp", "frame"), "tensor"),
            P(("dp", "frame"), "tensor"),
            P(("dp", "frame"), None, "tensor"),
        ),
        out_specs=(
            P("dp", ("frame", "tensor"), None, None),
            P("dp", ("frame", "tensor"), None, None),
            P(("dp", "frame"), None, "tensor"),
            P(("dp", "frame"), "tensor"),
            P(("dp", "frame"), "tensor"),
            P(("dp", "frame"), "tensor"),
            P(("dp", "frame"), None, "tensor"),
        ),
        check_vma=False,
    )
```

profile of v0, /device:TPU:0, one launch (start us, length us, event | category | flops | bytes accessed | tf_op | source)
XLA Modules:
  0.0 1416.2 jit_solution(16636748688124716342)
XLA Ops:
  24.1 50.8 %all-reduce.3.cloned.1.call-done = f32[8,2,4,6,256]{4,2,3,1,0:T(4,128)} async-done(((f32[8,2,4,6,256]{4,2,3,1,0:T(4,128)}), f32[8,2,4,6,256]{4,2,3,1,0:T(4,128)}) %all-reduce.3.cloned.1.call-update) | async-done | bytes 393232
  89.4 12.3 all-gather.16.cloned.1.call-done
  101.8 82.9 %all-gather.14.cloned.1.call-done = bf16[2,1024,1024]{2,1,0:T(8,128)(2,1)} async-done(((bf16[2,256,1024]{2,1,0:T(8,128)(2,1)}), bf16[2,1024,1024]{2,1,0:T(8,128)(2,1)}) %all-gather.14.cloned.1.call-update) | async-done | bytes 4194320 | tf_op jit(solution)/shard_map/forward/all_gather | solution.py:76
  217.8 87.8 %while.27 = (s32[]{:T(128)}, bf16[2,2,512,4,64]{2,4,3,1,0:T(8,128)(2,1)}, f32[2,2,4,512]{3,2,1,0:T(4,128)S(1)}, bf16[2,2,512,4,64]{2,4,3,1,0:T(8,128)(2,1)}, bf1...) while((s32[]{:T(128)}, bf16[2,2,512,4,64]{2,4,3,1,0:T(8,128)(2,1)}, ...), condition=%wide.region_6.7_spmd, body=%wide.region_3.6_spmd.sunk | while | flops 2223239168 | bytes 106037344 | solution.py:118
  217.8 14.3 %multiply_reduce_fusion.5 = (f32[2,4,512]{2,1,0:T(4,128)S(1)}, f32[2,4,512,2048]{3,2,1,0:T(8,128)}) fusion(bf16[2,2048,4,64]{1,3,2,0:T(8,128)(2,1)S(1)} %get-tuple-element.435, bf16[2,2,512,4,64]{2,4,3,1,0:T(8,128)(2,1)} %get-tuple-element.434, s32[]{:T(128)S(6)} %copy.212), kind=kOutput, calls=%fused_computation.2.clone.1 | convolution fusion | flops 1090514944 | bytes 36192260 | tf_op jit(solution)/shard_map/forward/while/body/eval_jaxpr/cqhe,ckhe->chqk/dot_general | solution.py:104
  232.1 14.0 fusion.138
  246.1 15.5 %fusion.139 = bf16[2,2,512,4,64]{2,4,3,1,0:T(8,128)(2,1)} fusion(bf16[2,2,512,4,64]{2,4,3,1,0:T(8,128)(2,1)} %get-tuple-element.425, s32[]{:T(128)S(6)} %copy.212, bf16[2,2048,4,64]{1,3,2,0:T(8,128)(2,1)} %get-tuple-element.436, f32[2,4,512,2048]{3,2,1,0:T(8,128)} %get-tuple-element.404, f32[2,4,512]{2,1,0:T(4,128)S(1)} %fusion.138, ...), kind=kOutput, calls=%fused_computation.7.clone.1 | convolution fusion | flops 1107558400 | bytes 36208644 | tf_op jit(solution)/shard_map/forward/while/body/eval_jaxpr/chqk,ckhe->cqhe/dot_general | solution.py:113
  261.7 14.3 %multiply_reduce_fusion.5 = (f32[2,4,512]{2,1,0:T(4,128)S(1)}, f32[2,4,512,2048]{3,2,1,0:T(8,128)}) fusion(bf16[2,2048,4,64]{1,3,2,0:T(8,128)(2,1)S(1)} %get-tuple-element.435, bf16[2,2,512,4,64]{2,4,3,1,0:T(8,128)(2,1)} %get-tuple-element.434, s32[]{:T(128)S(6)} %copy.212), kind=kOutput, calls=%fused_computation.2.clone.1 | convolution fusion | flops 1090514944 | bytes 36192260 | tf_op jit(solution)/shard_map/forward/while/body/eval_jaxpr/cqhe,ckhe->chqk/dot_general | solution.py:104
  276.0 14.0 fusion.138
  290.0 15.5 %fusion.139 = bf16[2,2,512,4,64]{2,4,3,1,0:T(8,128)(2,1)} fusion(bf16[2,2,512,4,64]{2,4,3,1,0:T(8,128)(2,1)} %get-tuple-element.425, s32[]{:T(128)S(6)} %copy.212, bf16[2,2048,4,64]{1,3,2,0:T(8,128)(2,1)} %get-tuple-element.436, f32[2,4,512,2048]{3,2,1,0:T(8,128)} %get-tuple-element.404, f32[2,4,512]{2,1,0:T(4,128)S(1)} %fusion.138, ...), kind=kOutput, calls=%fused_computation.7.clone.1 | convolution fusion | flops 1107558400 | bytes 36208644 | tf_op jit(solution)/shard_map/forward/while/body/eval_jaxpr/chqk,ckhe->cqhe/dot_general | solution.py:113
  317.2 76.9 %reduce-scatter.11.cloned.1.call-done = bf16[2,256,1024]{2,1,0:T(8,128)(2,1)} async-done(((bf16[2,1024,1024]{2,1,0:T(8,128)(2,1)}), bf16[2,256,1024]{2,1,0:T(8,128)(2,1)}) %reduce-scatter.11.cloned.1.call-update) | async-done | bytes 1048592 | tf_op jit(solution)/shard_map/forward/reduce_scatter | solution.py:79
  404.6 19.7 %all-gather.20.cloned.1.call-done = bf16[1024,1024]{1,0:T(8,128)(2,1)} async-done(((bf16[128,1024]{1,0:T(8,128)(2,1)}), bf16[1024,1024]{1,0:T(8,128)(2,1)}) %all-gather.20.cloned.1.call-update) | async-done | bytes 2097168 | tf_op jit(solution)/shard_map/weights/all_gather | solution.py:67
  424.3 82.9 %all-gather.18.cloned.1.call-done = bf16[2,1024,1024]{2,1,0:T(8,128)(2,1)} async-done(((bf16[2,256,1024]{2,1,0:T(8,128)(2,1)}), bf16[2,1024,1024]{2,1,0:T(8,128)(2,1)}) %all-gather.18.cloned.1.call-update) | async-done | bytes 4194320 | tf_op jit(solution)/shard_map/forward/all_gather | solution.py:76
  517.9 17.6 %all-gather.22.cloned.1.call-done = bf16[1024,1024]{1,0:T(8,128)(2,1)} async-done(((bf16[128,1024]{1,0:T(8,128)(2,1)}), bf16[1024,1024]{1,0:T(8,128)(2,1)}) %all-gather.22.cloned.1.call-update) | async-done | bytes 2097168 | tf_op jit(solution)/shard_map/weights/all_gather | solution.py:67
  535.4 82.2 %all-gather.24.cloned.1.call-done = bf16[2,1024,1024]{2,1,0:T(8,128)(2,1)} async-done(((bf16[2,256,1024]{2,1,0:T(8,128)(2,1)}), bf16[2,1024,1024]{2,1,0:T(8,128)(2,1)}) %all-gather.24.cloned.1.call-update) | async-done | bytes 4194320 | tf_op jit(solution)/shard_map/backward_ffn/all_gather | solution.py:76
  617.6 12.5 fusion.40
  638.7 75.2 %reduce-scatter.15.cloned.1.call-done = bf16[2,256,1024]{2,1,0:T(8,128)(2,1)} async-done(((bf16[2,1024,1024]{2,1,0:T(8,128)(2,1)}), bf16[2,256,1024]{2,1,0:T(8,128)(2,1)}) %reduce-scatter.15.cloned.1.call-update) | async-done | bytes 1048592 | tf_op jit(solution)/shard_map/backward_ffn/reduce_scatter | solution.py:79
  721.0 81.3 %all-gather.26.cloned.1.call-done = bf16[2,1024,1024]{2,1,0:T(8,128)(2,1)} async-done(((bf16[2,256,1024]{2,1,0:T(8,128)(2,1)}), bf16[2,1024,1024]{2,1,0:T(8,128)(2,1)}) %all-gather.26.cloned.1.call-update) | async-done | bytes 4194320 | tf_op jit(solution)/shard_map/backward_attention/all_gather | solution.py:76
  814.1 200.8 %while.28 = (s32[]{:T(128)}, f32[2,2048,4,64]{1,3,2,0:T(8,128)}, f32[2,2048,4,64]{1,3,2,0:T(8,128)}, bf16[2,2,512,4,64]{2,4,3,1,0:T(8,128)(2,1)}, bf16[2,2,512,4...) while((s32[]{:T(128)}, f32[2,2048,4,64]{1,3,2,0:T(8,128)}, ...), condition=%wide.region_16.17_spmd.clone, body=%wide.region_14.16_spmd.clone.sunk | while | flops 5474873344 | bytes 345096384 | solution.py:210
  814.1 14.3 %fusion.149 = f32[2,4,512,2048]{3,2,1,0:T(8,128)} fusion(bf16[2,2048,4,64]{1,3,2,0:T(8,128)(2,1)S(1)} %get-tuple-element.465, bf16[2,2,512,4,64]{2,4,3,1,0:T(8,128)(2,1)} %get-tuple-element.464, s32[]{:T(128)S(6)} %copy.222), kind=kOutput, calls=%fused_computation.30.clone.1 | convolution fusion | flops 1073741824 | bytes 36175876 | tf_op jit(solution)/shard_map/backward_attention/while/body/eval_jaxpr/cqhe,ckhe->chqk/dot_general | solution.py:177
  828.4 16.1 %bitcast_add_fusion.5 = f32[2,2048,4,64]{1,3,2,0:T(8,128)} fusion(f32[2,2048,4,64]{1,3,2,0:T(8,128)} %get-tuple-element.451, f32[2,4,512,2048]{3,2,1,0:T(8,128)} %fusion.149, f32[2,4,512]{2,1,0:T(4,128)S(1)} %dynamic-slice_bitcast_fusion.3, pred[]{:T(512)S(6)} %compare.3, bf16[2,2,512,4,64]{2,4,3,1,0:T(8,128)(2,1)} %get-tuple-element.467, s32[]{:T(128)S(6)} %copy.222), kind=kOutput, calls=%fused_computation.21.clone.1 | convolution fusion | flops 1101004800 | bytes 42483716 | tf_op jit(solution)/shard_map/backward_attention/while/body/eval_jaxpr/chqk,cqhe->ckhe/dot_general | solution.py:186
  844.4 23.8 %multiply_reduce_fusion.6 = (f32[2,4,512]{2,1,0:T(4,128)S(1)}, f32[2,4,512,2048]{3,2,1,0:T(8,128)}) fusion(f32[2,4,512,2048]{3,2,1,0:T(8,128)} %fusion.149, f32[2,4,512]{2,1,0:T(4,128)S(1)} %dynamic-slice_bitcast_fusion.3, bf16[2,2048,4,64]{1,3,2,0:T(8,128)(2,1)} %get-tuple-element.468, bf16[2,2,512,4,64]{2,4,3,1,0:T(8,128)(2,1)} %get-tuple-element.467, ...), kind=kOutput, calls=%fused_computation.15.clone.1 | convolution fusion | flops 1107292160 | bytes 69763072 | tf_op jit(solution)/shard_map/backward_attention/while/body/eval_jaxpr/cqhe,ckhe->chqk/dot_general | solution.py:183
  868.2 27.9 %multiply_convert_fusion.7 = bf16[2,4,512,2048]{3,2,1,0:T(8,128)(2,1)} fusion(f32[2,4,512,2048]{3,2,1,0:T(8,128)} %get-tuple-element.415, f32[2,4,512,2048]{3,2,1,0:T(8,128)} %fusion.149, f32[2,4,512]{2,1,0:T(4,128)S(1)} %get-tuple-element.416, f32[2,4,512]{2,1,0:T(4,128)S(1)} %dynamic-slice_bitcast_fusion.3), kind=kLoop, calls=%fused_computation.14.clone.1 | loop fusion | flops 41943040 | bytes 83918848 | tf_op jit(solution)/shard_map/backward_attention/while/body/eval_jaxpr/convert_element_type | solution.py:193
  913.0 14.3 %fusion.149 = f32[2,4,512,2048]{3,2,1,0:T(8,128)} fusion(bf16[2,2048,4,64]{1,3,2,0:T(8,128)(2,1)S(1)} %get-tuple-element.465, bf16[2,2,512,4,64]{2,4,3,1,0:T(8,128)(2,1)} %get-tuple-element.464, s32[]{:T(128)S(6)} %copy.222), kind=kOutput, calls=%fused_computation.30.clone.1 | convolution fusion | flops 1073741824 | bytes 36175876 | tf_op jit(solution)/shard_map/backward_attention/while/body/eval_jaxpr/cqhe,ckhe->chqk/dot_general | solution.py:177
  927.3 17.2 %bitcast_add_fusion.5 = f32[2,2048,4,64]{1,3,2,0:T(8,128)} fusion(f32[2,2048,4,64]{1,3,2,0:T(8,128)} %get-tuple-element.451, f32[2,4,512,2048]{3,2,1,0:T(8,128)} %fusion.149, f32[2,4,512]{2,1,0:T(4,128)S(1)} %dynamic-slice_bitcast_fusion.3, pred[]{:T(512)S(6)} %compare.3, bf16[2,2,512,4,64]{2,4,3,1,0:T(8,128)(2,1)} %get-tuple-element.467, s32[]{:T(128)S(6)} %copy.222), kind=kOutput, calls=%fused_computation.21.clone.1 | convolution fusion | flops 1101004800 | bytes 42483716 | tf_op jit(solution)/shard_map/backward_attention/while/body/eval_jaxpr/chqk,cqhe->ckhe/dot_general | solution.py:186
  944.6 23.9 %multiply_reduce_fusion.6 = (f32[2,4,512]{2,1,0:T(4,128)S(1)}, f32[2,4,512,2048]{3,2,1,0:T(8,128)}) fusion(f32[2,4,512,2048]{3,2,1,0:T(8,128)} %fusion.149, f32[2,4,512]{2,1,0:T(4,128)S(1)} %dynamic-slice_bitcast_fusion.3, bf16[2,2048,4,64]{1,3,2,0:T(8,128)(2,1)} %get-tuple-element.468, bf16[2,2,512,4,64]{2,4,3,1,0:T(8,128)(2,1)} %get-tuple-element.467, ...), kind=kOutput, calls=%fused_computation.15.clone.1 | convolution fusion | flops 1107292160 | bytes 69763072 | tf_op jit(solution)/shard_map/backward_attention/while/body/eval_jaxpr/cqhe,ckhe->chqk/dot_general | solution.py:183
  968.4 27.9 %multiply_convert_fusion.7 = bf16[2,4,512,2048]{3,2,1,0:T(8,128)(2,1)} fusion(f32[2,4,512,2048]{3,2,1,0:T(8,128)} %get-tuple-element.415, f32[2,4,512,2048]{3,2,1,0:T(8,128)} %fusion.149, f32[2,4,512]{2,1,0:T(4,128)S(1)} %get-tuple-element.416, f32[2,4,512]{2,1,0:T(4,128)S(1)} %dynamic-slice_bitcast_fusion.3), kind=kLoop, calls=%fused_computation.14.clone.1 | loop fusion | flops 41943040 | bytes 83918848 | tf_op jit(solution)/shard_map/backward_attention/while/body/eval_jaxpr/convert_element_type | solution.py:193
  1089.0 42.5 %reduce-scatter.27.cloned.1.call-done = bf16[128,1024]{1,0:T(8,128)(2,1)} async-done(((bf16[1024,1024]{1,0:T(8,128)(2,1)}), bf16[128,1024]{1,0:T(8,128)(2,1)}) %reduce-scatter.27.cloned.1.call-update) | async-done | bytes 262160 | tf_op jit(solution)/shard_map/weight_grads/reduce_scatter | solution.py:259
  1133.3 35.9 %reduce-scatter.25.cloned.1.call-done = bf16[128,256]{1,0:T(8,128)(2,1)} async-done(((bf16[1024,256]{1,0:T(8,128)(2,1)}), bf16[128,256]{1,0:T(8,128)(2,1)}) %reduce-scatter.25.cloned.1.call-update) | async-done | bytes 65552 | tf_op jit(solution)/shard_map/weight_grads/reduce_scatter | solution.py:259
  1170.7 40.0 %reduce-scatter.23.cloned.1.call-done = bf16[128,3,256]{2,0,1:T(8,128)(2,1)} async-done(((bf16[1024,3,256]{2,0,1:T(8,128)(2,1)}), bf16[128,3,256]{2,0,1:T(8,128)(2,1)}) %reduce-scatter.23.cloned.1.call-update) | async-done | bytes 196624 | tf_op jit(solution)/shard_map/weight_grads/reduce_scatter | solution.py:259
  1212.4 77.4 %reduce-scatter.13.cloned.1.call-done = bf16[2,256,1024]{2,1,0:T(8,128)(2,1)} async-done(((bf16[2,1024,1024]{2,1,0:T(8,128)(2,1)}), bf16[2,256,1024]{2,1,0:T(8,128)(2,1)}) %reduce-scatter.13.cloned.1.call-update) | async-done | bytes 1048592 | tf_op jit(solution)/shard_map/forward/reduce_scatter | solution.py:79
  1289.8 79.5 %reduce-scatter.21.cloned.1.call-done = bf16[2,256,1024]{2,1,0:T(8,128)(2,1)} async-done(((bf16[2,1024,1024]{2,1,0:T(8,128)(2,1)}), bf16[2,256,1024]{2,1,0:T(8,128)(2,1)}) %reduce-scatter.21.cloned.1.call-update) | async-done | bytes 1048592 | tf_op jit(solution)/shard_map/backward_attention/reduce_scatter | solution.py:79
  (221 shorter events, 277.9 us)
Async XLA Ops:
  7.2 67.7 %all-reduce.3.cloned.1.call-start = ((), (), s32[]{:S(2)}) async-start(), calls=%async_computation.31 | async-start | bytes 786432
  20.2 81.6 %all-gather.16.cloned.1.call-start = ((), (), s32[]{:S(2)}) async-start(), calls=%async_computation.13 | async-start | bytes 1769472 | tf_op jit(solution)/shard_map/weights/all_gather | solution.py:67
  77.0 10.2 all-to-all-start
  81.5 103.1 %all-gather.14.cloned.1.call-start = ((), (), s32[]{:S(2)}) async-start(), calls=%async_computation.12 | async-start | bytes 5242880 | tf_op jit(solution)/shard_map/forward/all_gather | solution.py:76
  89.4 117.2 %all-gather.30.cloned.1.call-start = ((), (), s32[]{:S(2)}) async-start(), calls=%async_computation.30 | async-start | bytes 3145728 | tf_op jit(solution)/shard_map/forward/all_gather | solution.py:93
  192.4 22.4 %all-gather.28.cloned.1.call-start = ((), (), s32[]{:S(2)}) async-start(), calls=%async_computation.29 | async-start | bytes 3145728 | tf_op jit(solution)/shard_map/forward/all_gather | solution.py:92
  193.0 201.1 %reduce-scatter.11.cloned.1.call-start = ((), (), s32[]{:S(2)}) async-start(), calls=%async_computation.14 | async-start | bytes 5242880 | tf_op jit(solution)/shard_map/forward/reduce_scatter | solution.py:79
  316.0 108.3 %all-gather.20.cloned.1.call-start = ((), (), s32[]{:S(2)}) async-start(), calls=%async_computation.16 | async-start | bytes 2359296 | tf_op jit(solution)/shard_map/weights/all_gather | solution.py:67
  316.8 190.5 %all-gather.18.cloned.1.call-start = ((), (), s32[]{:S(2)}) async-start(), calls=%async_computation.15 | async-start | bytes 5242880 | tf_op jit(solution)/shard_map/forward/all_gather | solution.py:76
  396.2 320.6 %copy-start.19 = (f32[2,256]{1,0:T(2,128)}, f32[2,256]{1,0:T(2,128)S(1)}, u32[]{:S(2)}) copy-start(f32[2,256]{1,0:T(2,128)S(1)} %broadcast_multiply_fusion.4) | copy-start | bytes 6148
  398.3 318.4 %copy-start.21 = (f32[2,256]{1,0:T(2,128)}, f32[2,256]{1,0:T(2,128)S(1)}, u32[]{:S(2)}) copy-start(f32[2,256]{1,0:T(2,128)S(1)} %add_rsqrt_fusion) | copy-start | bytes 6148
  401.2 134.2 %all-gather.22.cloned.1.call-start = ((), (), s32[]{:S(2)}) async-start(), calls=%async_computation.17 | async-start | bytes 2359296 | tf_op jit(solution)/shard_map/weights/all_gather | solution.py:67
  402.0 215.7 %all-gather.24.cloned.1.call-start = ((), (), s32[]{:S(2)}) async-start(), calls=%async_computation.19 | async-start | bytes 5242880 | tf_op jit(solution)/shard_map/backward_ffn/all_gather | solution.py:76
  404.6 309.3 %reduce-scatter.15.cloned.1.call-start = ((), (), s32[]{:S(2)}) async-start(), calls=%async_computation.20 | async-start | bytes 5242880 | tf_op jit(solution)/shard_map/backward_ffn/reduce_scatter | solution.py:79
  638.5 163.8 %all-gather.26.cloned.1.call-start = ((), (), s32[]{:S(2)}) async-start(), calls=%async_computation.21 | async-start | bytes 5242880 | tf_op jit(solution)/shard_map/backward_attention/all_gather | solution.py:76
  720.9 335.7 %reduce-scatter.17.cloned.1.call-start = ((), (), s32[]{:S(2)}) async-start(), calls=%async_computation.22 | async-start | bytes 3145728 | tf_op jit(solution)/shard_map/backward_attention/reduce_scatter | solution.py:215
  1020.0 36.7 %reduce-scatter.19.cloned.1.call-start = ((), (), s32[]{:S(2)}) async-start(), calls=%async_computation.23 | async-start | bytes 3145728 | tf_op jit(solution)/shard_map/backward_attention/reduce_scatter | solution.py:215
  1025.1 62.1 %reduce-scatter.29.cloned.1.call-start = ((), (), s32[]{:S(2)}) async-start(), calls=%async_computation.28 | async-start | bytes 2359296 | tf_op jit(solution)/shard_map/weight_grads/reduce_scatter | solution.py:259
  1036.4 95.1 %reduce-scatter.27.cloned.1.call-start = ((), (), s32[]{:S(2)}) async-start(), calls=%async_computation.27 | async-start | bytes 2359296 | tf_op jit(solution)/shard_map/weight_grads/reduce_scatter | solution.py:259
  1046.5 122.6 %reduce-scatter.25.cloned.1.call-start = ((), (), s32[]{:S(2)}) async-start(), calls=%async_computation.26 | async-start | bytes 589824 | tf_op jit(solution)/shard_map/weight_grads/reduce_scatter | solution.py:259
  1056.6 154.1 %reduce-scatter.23.cloned.1.call-start = ((), (), s32[]{:S(2)}) async-start(), calls=%async_computation.25 | async-start | bytes 1769472 | tf_op jit(solution)/shard_map/weight_grads/reduce_scatter | solution.py:259
  1064.5 225.4 %reduce-scatter.13.cloned.1.call-start = ((), (), s32[]{:S(2)}) async-start(), calls=%async_computation.18 | async-start | bytes 5242880 | tf_op jit(solution)/shard_map/forward/reduce_scatter | solution.py:79
  1076.3 293.0 %reduce-scatter.21.cloned.1.call-start = ((), (), s32[]{:S(2)}) async-start(), calls=%async_computation.24 | async-start | bytes 5242880 | tf_op jit(solution)/shard_map/backward_attention/reduce_scatter | solution.py:79
  1084.5 284.8 %copy-start.13 = (f32[2,1024]{1,0:T(2,128)S(1)}, f32[2,1024]{1,0:T(2,128)}, u32[]{:S(2)}) copy-start(f32[2,1024]{1,0:T(2,128)} %get-tuple-element.312) | copy-start | bytes 24580
  1084.5 284.8 %copy-start.15 = (f32[2,1024]{1,0:T(2,128)S(1)}, f32[2,1024]{1,0:T(2,128)}, u32[]{:S(2)}) copy-start(f32[2,1024]{1,0:T(2,128)} %get-tuple-element.309) | copy-start | bytes 24580
  1084.5 284.8 %copy-start.18 = (f32[2,1024]{1,0:T(2,128)S(1)}, f32[2,1024]{1,0:T(2,128)}, u32[]{:S(2)}) copy-start(f32[2,1024]{1,0:T(2,128)} %copy-done.17) | copy-start | bytes 24580
  1084.5 284.8 %copy-start.20 = (f32[2,256]{1,0:T(2,128)S(1)}, f32[2,256]{1,0:T(2,128)}, u32[]{:S(2)}) copy-start(f32[2,256]{1,0:T(2,128)} %copy-done.19) | copy-start | bytes 6148
  1084.5 284.8 %copy-start.22 = (f32[2,256]{1,0:T(2,128)S(1)}, f32[2,256]{1,0:T(2,128)}, u32[]{:S(2)}) copy-start(f32[2,256]{1,0:T(2,128)} %copy-done.21) | copy-start | bytes 6148
  1084.5 284.8 %copy-start.24 = (f32[2,1024]{1,0:T(2,128)S(1)}, f32[2,1024]{1,0:T(2,128)}, u32[]{:S(2)}) copy-start(f32[2,1024]{1,0:T(2,128)} %get-tuple-element.307) | copy-start | bytes 24580
  1084.5 284.8 %copy-start.27 = (f32[2,256]{1,0:T(2,128)S(1)}, f32[2,256]{1,0:T(2,128)}, u32[]{:S(2)}) copy-start(f32[2,256]{1,0:T(2,128)} %copy-done.26) | copy-start | bytes 6148
  1084.6 284.8 %copy-start.29 = (f32[2,256]{1,0:T(2,128)S(1)}, f32[2,256]{1,0:T(2,128)}, u32[]{:S(2)}) copy-start(f32[2,256]{1,0:T(2,128)} %copy-done.28) | copy-start | bytes 6148
  1383.3 10.0 all-to-all-start.1
  (30 other events, 2165.0 us)
Sparse Core Ops, SparseCore 0:
  20.3 54.5 all-reduce.2
  76.8 24.9 all-gather.15
  103.9 80.7 all-gather.13
  192.5 9.1 all-gather.29
  203.1 11.7 all-gather.27
  316.1 77.9 reduce-scatter.10
  396.0 28.2 all-gather.19
  426.5 80.7 all-gather.17
  509.1 26.2 all-gather.21
  536.9 80.7 all-gather.23
  638.6 75.2 reduce-scatter.14
  721.0 81.2 all-gather.25
  1020.1 8.3 reduce-scatter.16
  1030.6 11.0 reduce-scatter.18
  1044.8 42.3 reduce-scatter.28
  1090.3 41.1 reduce-scatter.26
  1135.0 34.1 reduce-scatter.24
  1172.3 38.3 reduce-scatter.22
  1213.0 76.7 reduce-scatter.12
  1292.0 77.2 reduce-scatter.20
where the time goes:
time: 1420 us
  waiting for transfers between devices  874 us (62%)
  matrix products  302 us (21%)
  other arithmetic  129 us (9%)
  local copies, waits for them, and re-layouts  53.9 us (4%)
  blocking collectives  31.3 us (2%)
  between operations  15.2 us (1%)
    all_gather x4, waiting for transfers between devices, gather_tokens(): return lax.all_gather(values, 'tensor', axis=1, tiled=True)  329 us
    reduce_scatter x4, waiting for transfers between devices, scatter_tokens(): lax.psum_scatter(values.astype(jnp.bfloat16), 'tensor', scatter_dimension...  309 us
    reduce_scatter x4, waiting for transfers between devices, on_device(): lax.psum_scatter(total.astype(jnp.bfloat16), ('dp', 'frame'), scatter_dim...  121 us
    convert_element_type x2, other arithmetic, attend_back(): grad_scores = (probs * (grad_probs - row_terms)).astype(jnp.bfloat16)  55.8 us
    unnamed x21, waiting for transfers between devices  53.7 us
    all_gather x3, waiting for transfers between devices, on_device(): lax.all_gather(w, ('dp', 'frame'), axis=0, tiled=True)  49.6 us
    dot_general x2, matrix products, attend_back(): jnp.einsum('cqhe,ckhe->chqk', grad_block, value_heads, preferred_element_...  47.7 us
    dot_general x2, matrix products, attend_back(): jnp.einsum('chqk,cqhe->ckhe', probs.astype(jnp.bfloat16), grad_block, pre...  33.3 us
  transfers between devices with their start and end apart: 22, of which 19 were waited for; matrix products, arithmetic and copies ran while one was open for 8% of the time, Pallas kernels for 0%

commit v1 on v0

--- a/solution.py
+++ b/solution.py
@@ -3,6 +3,7 @@
 import jax.numpy as jnp
 from jax import lax
 from jax.sharding import PartitionSpec as P
+from jax.lax import axis_index, axis_size, ppermute
 
 HEAD_DIM = 64
 epsilon = 1e-06
@@ -63,8 +64,35 @@
         modulation = lax.all_to_all(summed_mod, "tensor", 1, 3, tiled=True)
         modulation = modulation.reshape(clips, 6, 1, model_width)
     with jax.named_scope("weights"):
+
+        def handle_desk(along_axis, my_data):
+            carry, view_out, x_next = (
+                axis_size(along_axis),
+                axis_index(along_axis),
+                my_data.shape[0],
+            )
+            y_new = lax.dynamic_update_slice_in_dim(
+                jnp.zeros(
+                    [i0 * carry if dev == 0 else i0 for dev, i0 in enumerate(my_data.shape)],
+                    my_data.dtype,
+                ),
+                my_data,
+                view_out * x_next,
+                axis=0,
+            )
+            for kk in range(1, carry):
+                my_data = ppermute(
+                    my_data,
+                    along_axis,
+                    list(map(lambda dev: (dev, (dev + 1) % carry), range(carry))),
+                )
+                y_new = lax.dynamic_update_slice_in_dim(
+                    y_new, my_data, (view_out - kk) % carry * x_next, axis=0
+                )
+            return y_new
+
         joint_weight, mixer_weight, upward_weight, downward_weight = (
-            lax.all_gather(w, ("dp", "frame"), axis=0, tiled=True)
+            handle_desk(("dp", "frame"), my_data=w)
             for w in (qkv_weight, out_weight, up_weight, down_weight)
         )
     residual = tokens[:, 0].astype(jnp.float32)

time: 1420 us -> 1370 us (0.965)
  waiting for transfers between devices: 874 us -> 812 us
  local copies, waits for them, and re-layouts: 53.9 us -> 68.8 us
    all_gather x4, waiting for transfers between devices: 329 us -> 215 us  [gather_tokens(): return lax.all_gather(values, 'tensor', axis=1, tiled=True)]
    ppermute x0 -> x28, waiting for transfers between devices: none -> 108 us  [handle_desk(): ppermute(my_data, along_axis, list(map(lambda dev: (dev, (dev + 1) % carr...]
    all_gather x3 -> x0, waiting for transfers between devices: 49.6 us -> none  [on_device(): lax.all_gather(w, ('dp', 'frame'), axis=0, tiled=True)]
    unnamed x21 -> x18, waiting for transfers between devices: 53.7 us -> 54.2 us
  transfers between devices with their start and end apart: 22 -> 47, of which waited for: 19 -> 42; matrix products, arithmetic and copies ran while one was open for 8% -> 8% of each run, Pallas kernels for 0% -> 0%
where the time goes in v1:
time: 1370 us; the launch traced here: 1360 us
  waiting for transfers between devices  812 us (59%)
  matrix products  302 us (22%)
  other arithmetic  126 us (9%)
  local copies, waits for them, and re-layouts  68.8 us (5%)
  blocking collectives  20.2 us (1%)
  between operations  15 us (1%)
    reduce_scatter x4, waiting for transfers between devices, scatter_tokens(): lax.psum_scatter(values.astype(jnp.bfloat16), 'tensor', scatter_dimension...  306 us
    all_gather x4, waiting for transfers between devices, gather_tokens(): return lax.all_gather(values, 'tensor', axis=1, tiled=True)  215 us
    reduce_scatter x4, waiting for transfers between devices, on_device(): lax.psum_scatter(total.astype(jnp.bfloat16), ('dp', 'frame'), scatter_dim...  122 us
    ppermute x28, waiting for transfers between devices, handle_desk(): ppermute(my_data, along_axis, list(map(lambda dev: (dev, (dev + 1) % carr...  108 us
    convert_element_type x2, other arithmetic, attend_back(): grad_scores = (probs * (grad_probs - row_terms)).astype(jnp.bfloat16)  55.8 us
    unnamed x18, waiting for transfers between devices  54.2 us
    dot_general x2, matrix products, attend_back(): jnp.einsum('cqhe,ckhe->chqk', grad_block, value_heads, preferred_element_...  47.7 us
    dot_general x2, matrix products, attend_back(): jnp.einsum('chqk,cqhe->ckhe', probs.astype(jnp.bfloat16), grad_block, pre...  33.3 us
  transfers between devices with their start and end apart: 47, of which 42 were waited for; matrix products, arithmetic and copies ran while one was open for 8% of the time, Pallas kernels for 0%

profile of v1, /device:TPU:0, one launch (start us, length us, event | category | flops | bytes accessed | tf_op | source)
XLA Modules:
  0.0 1357.4 jit_solution(7343074640658983733)
XLA Ops:
  21.5 53.5 %all-reduce.3.cloned.1.call-done = f32[8,2,4,6,256]{4,2,3,1,0:T(4,128)} async-done(((f32[8,2,4,6,256]{4,2,3,1,0:T(4,128)}), f32[8,2,4,6,256]{4,2,3,1,0:T(4,128)}) %all-reduce.3.cloned.1.call-update) | async-done | bytes 393232
  131.6 35.7 %all-gather.11.cloned.1.call-done = bf16[2,1024,1024]{2,1,0:T(8,128)(2,1)} async-done(((bf16[2,256,1024]{2,1,0:T(8,128)(2,1)}), bf16[2,1024,1024]{2,1,0:T(8,128)(2,1)}) %all-gather.11.cloned.1.call-update) | async-done | bytes 4194320 | tf_op jit(solution)/shard_map/forward/all_gather | solution.py:104
  217.8 87.8 %while.27 = (s32[]{:T(128)}, bf16[2,2,512,4,64]{2,4,3,1,0:T(8,128)(2,1)}, f32[2,2,4,512]{3,2,1,0:T(4,128)S(1)}, bf16[2,2,512,4,64]{2,4,3,1,0:T(8,128)(2,1)}, bf1...) while((s32[]{:T(128)}, bf16[2,2,512,4,64]{2,4,3,1,0:T(8,128)(2,1)}, ...), condition=%wide.region_6.7_spmd, body=%wide.region_3.6_spmd.sunk | while | flops 2223239168 | bytes 106037344 | solution.py:146
  217.8 14.3 %multiply_reduce_fusion.5 = (f32[2,4,512]{2,1,0:T(4,128)S(1)}, f32[2,4,512,2048]{3,2,1,0:T(8,128)}) fusion(bf16[2,2048,4,64]{1,3,2,0:T(8,128)(2,1)S(1)} %get-tuple-element.435, bf16[2,2,512,4,64]{2,4,3,1,0:T(8,128)(2,1)} %get-tuple-element.434, s32[]{:T(128)S(6)} %copy.220), kind=kOutput, calls=%fused_computation.2.clone.1 | convolution fusion | flops 1090514944 | bytes 36192260 | tf_op jit(solution)/shard_map/forward/while/body/eval_jaxpr/cqhe,ckhe->chqk/dot_general | solution.py:132
  232.1 14.0 %fusion.138 = f32[2,4,512]{2,1,0:T(4,128)S(1)} fusion(f32[2,4,512,2048]{3,2,1,0:T(8,128)} %get-tuple-element.404, f32[2,4,512]{2,1,0:T(4,128)S(1)} %get-tuple-element.405), kind=kLoop, calls=%fused_computation.3.clone.1 | loop fusion | flops 25161728 | bytes 33587200 | tf_op jit(solution)/shard_map/forward/while/body/eval_jaxpr/reduce_sum | solution.py:139
  246.2 15.5 %fusion.139 = bf16[2,2,512,4,64]{2,4,3,1,0:T(8,128)(2,1)} fusion(bf16[2,2,512,4,64]{2,4,3,1,0:T(8,128)(2,1)} %get-tuple-element.425, s32[]{:T(128)S(6)} %copy.220, bf16[2,2048,4,64]{1,3,2,0:T(8,128)(2,1)} %get-tuple-element.436, f32[2,4,512,2048]{3,2,1,0:T(8,128)} %get-tuple-element.404, f32[2,4,512]{2,1,0:T(4,128)S(1)} %fusion.138, ...), kind=kOutput, calls=%fused_computation.7.clone.1 | convolution fusion | flops 1107558400 | bytes 36208644 | tf_op jit(solution)/shard_map/forward/while/body/eval_jaxpr/chqk,ckhe->cqhe/dot_general | solution.py:141
  261.7 14.3 %multiply_reduce_fusion.5 = (f32[2,4,512]{2,1,0:T(4,128)S(1)}, f32[2,4,512,2048]{3,2,1,0:T(8,128)}) fusion(bf16[2,2048,4,64]{1,3,2,0:T(8,128)(2,1)S(1)} %get-tuple-element.435, bf16[2,2,512,4,64]{2,4,3,1,0:T(8,128)(2,1)} %get-tuple-element.434, s32[]{:T(128)S(6)} %copy.220), kind=kOutput, calls=%fused_computation.2.clone.1 | convolution fusion | flops 1090514944 | bytes 36192260 | tf_op jit(solution)/shard_map/forward/while/body/eval_jaxpr/cqhe,ckhe->chqk/dot_general | solution.py:132
  276.1 14.0 %fusion.138 = f32[2,4,512]{2,1,0:T(4,128)S(1)} fusion(f32[2,4,512,2048]{3,2,1,0:T(8,128)} %get-tuple-element.404, f32[2,4,512]{2,1,0:T(4,128)S(1)} %get-tuple-element.405), kind=kLoop, calls=%fused_computation.3.clone.1 | loop fusion | flops 25161728 | bytes 33587200 | tf_op jit(solution)/shard_map/forward/while/body/eval_jaxpr/reduce_sum | solution.py:139
  290.1 15.5 %fusion.139 = bf16[2,2,512,4,64]{2,4,3,1,0:T(8,128)(2,1)} fusion(bf16[2,2,512,4,64]{2,4,3,1,0:T(8,128)(2,1)} %get-tuple-element.425, s32[]{:T(128)S(6)} %copy.220, bf16[2,2048,4,64]{1,3,2,0:T(8,128)(2,1)} %get-tuple-element.436, f32[2,4,512,2048]{3,2,1,0:T(8,128)} %get-tuple-element.404, f32[2,4,512]{2,1,0:T(4,128)S(1)} %fusion.138, ...), kind=kOutput, calls=%fused_computation.7.clone.1 | convolution fusion | flops 1107558400 | bytes 36208644 | tf_op jit(solution)/shard_map/forward/while/body/eval_jaxpr/chqk,ckhe->cqhe/dot_general | solution.py:141
  316.5 74.1 %reduce-scatter.11.cloned.1.call-done = bf16[2,256,1024]{2,1,0:T(8,128)(2,1)} async-done(((bf16[2,1024,1024]{2,1,0:T(8,128)(2,1)}), bf16[2,256,1024]{2,1,0:T(8,128)(2,1)}) %reduce-scatter.11.cloned.1.call-update) | async-done | bytes 1048592 | tf_op jit(solution)/shard_map/forward/reduce_scatter | solution.py:107
  450.1 27.5 %all-gather.13.cloned.1.call-done = bf16[2,1024,1024]{2,1,0:T(8,128)(2,1)} async-done(((bf16[2,256,1024]{2,1,0:T(8,128)(2,1)}), bf16[2,1024,1024]{2,1,0:T(8,128)(2,1)}) %all-gather.13.cloned.1.call-update) | async-done | bytes 4194320 | tf_op jit(solution)/shard_map/forward/all_gather | solution.py:104
  477.7 10.8 fusion.81
  488.5 70.0 %all-gather.15.cloned.1.call-done = bf16[2,1024,1024]{2,1,0:T(8,128)(2,1)} async-done(((bf16[2,256,1024]{2,1,0:T(8,128)(2,1)}), bf16[2,1024,1024]{2,1,0:T(8,128)(2,1)}) %all-gather.15.cloned.1.call-update) | async-done | bytes 4194320 | tf_op jit(solution)/shard_map/backward_ffn/all_gather | solution.py:104
  558.5 12.4 fusion.40
  580.9 75.2 %reduce-scatter.15.cloned.1.call-done = bf16[2,256,1024]{2,1,0:T(8,128)(2,1)} async-done(((bf16[2,1024,1024]{2,1,0:T(8,128)(2,1)}), bf16[2,256,1024]{2,1,0:T(8,128)(2,1)}) %reduce-scatter.15.cloned.1.call-update) | async-done | bytes 1048592 | tf_op jit(solution)/shard_map/backward_ffn/reduce_scatter | solution.py:107
  663.1 81.3 %all-gather.17.cloned.1.call-done = bf16[2,1024,1024]{2,1,0:T(8,128)(2,1)} async-done(((bf16[2,256,1024]{2,1,0:T(8,128)(2,1)}), bf16[2,1024,1024]{2,1,0:T(8,128)(2,1)}) %all-gather.17.cloned.1.call-update) | async-done | bytes 4194320 | tf_op jit(solution)/shard_map/backward_attention/all_gather | solution.py:104
  756.3 200.8 %while.28 = (s32[]{:T(128)}, f32[2,2048,4,64]{1,3,2,0:T(8,128)}, f32[2,2048,4,64]{1,3,2,0:T(8,128)}, bf16[2,2,512,4,64]{2,4,3,1,0:T(8,128)(2,1)}, bf16[2,2,512,4...) while((s32[]{:T(128)}, f32[2,2048,4,64]{1,3,2,0:T(8,128)}, ...), condition=%wide.region_16.17_spmd.clone, body=%wide.region_14.16_spmd.clone.sunk | while | flops 5474873344 | bytes 345096384 | solution.py:238
  756.3 14.3 %fusion.149 = f32[2,4,512,2048]{3,2,1,0:T(8,128)} fusion(bf16[2,2048,4,64]{1,3,2,0:T(8,128)(2,1)S(1)} %get-tuple-element.465, bf16[2,2,512,4,64]{2,4,3,1,0:T(8,128)(2,1)} %get-tuple-element.464, s32[]{:T(128)S(6)} %copy.254), kind=kOutput, calls=%fused_computation.30.clone.1 | convolution fusion | flops 1073741824 | bytes 36175876 | tf_op jit(solution)/shard_map/backward_attention/while/body/eval_jaxpr/cqhe,ckhe->chqk/dot_general | solution.py:205
  770.5 16.0 %bitcast_add_fusion.5 = f32[2,2048,4,64]{1,3,2,0:T(8,128)} fusion(f32[2,2048,4,64]{1,3,2,0:T(8,128)} %get-tuple-element.451, f32[2,4,512,2048]{3,2,1,0:T(8,128)} %fusion.149, f32[2,4,512]{2,1,0:T(4,128)S(1)} %dynamic-slice_bitcast_fusion.3, pred[]{:T(512)S(6)} %compare.10, bf16[2,2,512,4,64]{2,4,3,1,0:T(8,128)(2,1)} %get-tuple-element.467, ...), kind=kOutput, calls=%fused_computation.21.clone.1 | convolution fusion | flops 1101004800 | bytes 42483716 | tf_op jit(solution)/shard_map/backward_attention/while/body/eval_jaxpr/chqk,cqhe->ckhe/dot_general | solution.py:214
  786.6 23.9 %multiply_reduce_fusion.6 = (f32[2,4,512]{2,1,0:T(4,128)S(1)}, f32[2,4,512,2048]{3,2,1,0:T(8,128)}) fusion(f32[2,4,512,2048]{3,2,1,0:T(8,128)} %fusion.149, f32[2,4,512]{2,1,0:T(4,128)S(1)} %dynamic-slice_bitcast_fusion.3, bf16[2,2048,4,64]{1,3,2,0:T(8,128)(2,1)} %get-tuple-element.468, bf16[2,2,512,4,64]{2,4,3,1,0:T(8,128)(2,1)} %get-tuple-element.467, ...), kind=kOutput, calls=%fused_computation.15.clone.1 | convolution fusion | flops 1107292160 | bytes 69763072 | tf_op jit(solution)/shard_map/backward_attention/while/body/eval_jaxpr/cqhe,ckhe->chqk/dot_general | solution.py:211
  810.5 27.9 %multiply_convert_fusion.7 = bf16[2,4,512,2048]{3,2,1,0:T(8,128)(2,1)} fusion(f32[2,4,512,2048]{3,2,1,0:T(8,128)} %get-tuple-element.415, f32[2,4,512,2048]{3,2,1,0:T(8,128)} %fusion.149, f32[2,4,512]{2,1,0:T(4,128)S(1)} %get-tuple-element.416, f32[2,4,512]{2,1,0:T(4,128)S(1)} %dynamic-slice_bitcast_fusion.3), kind=kLoop, calls=%fused_computation.14.clone.1 | loop fusion | flops 41943040 | bytes 83918848 | tf_op jit(solution)/shard_map/backward_attention/while/body/eval_jaxpr/convert_element_type | solution.py:221
  855.3 14.3 %fusion.149 = f32[2,4,512,2048]{3,2,1,0:T(8,128)} fusion(bf16[2,2048,4,64]{1,3,2,0:T(8,128)(2,1)S(1)} %get-tuple-element.465, bf16[2,2,512,4,64]{2,4,3,1,0:T(8,128)(2,1)} %get-tuple-element.464, s32[]{:T(128)S(6)} %copy.254), kind=kOutput, calls=%fused_computation.30.clone.1 | convolution fusion | flops 1073741824 | bytes 36175876 | tf_op jit(solution)/shard_map/backward_attention/while/body/eval_jaxpr/cqhe,ckhe->chqk/dot_general | solution.py:205
  869.6 17.2 %bitcast_add_fusion.5 = f32[2,2048,4,64]{1,3,2,0:T(8,128)} fusion(f32[2,2048,4,64]{1,3,2,0:T(8,128)} %get-tuple-element.451, f32[2,4,512,2048]{3,2,1,0:T(8,128)} %fusion.149, f32[2,4,512]{2,1,0:T(4,128)S(1)} %dynamic-slice_bitcast_fusion.3, pred[]{:T(512)S(6)} %compare.10, bf16[2,2,512,4,64]{2,4,3,1,0:T(8,128)(2,1)} %get-tuple-element.467, ...), kind=kOutput, calls=%fused_computation.21.clone.1 | convolution fusion | flops 1101004800 | bytes 42483716 | tf_op jit(solution)/shard_map/backward_attention/while/body/eval_jaxpr/chqk,cqhe->ckhe/dot_general | solution.py:214
  886.8 23.8 %multiply_reduce_fusion.6 = (f32[2,4,512]{2,1,0:T(4,128)S(1)}, f32[2,4,512,2048]{3,2,1,0:T(8,128)}) fusion(f32[2,4,512,2048]{3,2,1,0:T(8,128)} %fusion.149, f32[2,4,512]{2,1,0:T(4,128)S(1)} %dynamic-slice_bitcast_fusion.3, bf16[2,2048,4,64]{1,3,2,0:T(8,128)(2,1)} %get-tuple-element.468, bf16[2,2,512,4,64]{2,4,3,1,0:T(8,128)(2,1)} %get-tuple-element.467, ...), kind=kOutput, calls=%fused_computation.15.clone.1 | convolution fusion | flops 1107292160 | bytes 69763072 | tf_op jit(solution)/shard_map/backward_attention/while/body/eval_jaxpr/cqhe,ckhe->chqk/dot_general | solution.py:211
  910.6 27.9 %multiply_convert_fusion.7 = bf16[2,4,512,2048]{3,2,1,0:T(8,128)(2,1)} fusion(f32[2,4,512,2048]{3,2,1,0:T(8,128)} %get-tuple-element.415, f32[2,4,512,2048]{3,2,1,0:T(8,128)} %fusion.149, f32[2,4,512]{2,1,0:T(4,128)S(1)} %get-tuple-element.416, f32[2,4,512]{2,1,0:T(4,128)S(1)} %dynamic-slice_bitcast_fusion.3), kind=kLoop, calls=%fused_computation.14.clone.1 | loop fusion | flops 41943040 | bytes 83918848 | tf_op jit(solution)/shard_map/backward_attention/while/body/eval_jaxpr/convert_element_type | solution.py:221
  967.3 11.1 bitcast_convert_fusion.1
  1006.0 11.8 convolution_convert_fusion.1
  1031.2 42.6 %reduce-scatter.27.cloned.1.call-done = bf16[128,1024]{1,0:T(8,128)(2,1)} async-done(((bf16[1024,1024]{1,0:T(8,128)(2,1)}), bf16[128,1024]{1,0:T(8,128)(2,1)}) %reduce-scatter.27.cloned.1.call-update) | async-done | bytes 262160 | tf_op jit(solution)/shard_map/weight_grads/reduce_scatter | solution.py:287
  1075.6 35.9 %reduce-scatter.25.cloned.1.call-done = bf16[128,256]{1,0:T(8,128)(2,1)} async-done(((bf16[1024,256]{1,0:T(8,128)(2,1)}), bf16[128,256]{1,0:T(8,128)(2,1)}) %reduce-scatter.25.cloned.1.call-update) | async-done | bytes 65552 | tf_op jit(solution)/shard_map/weight_grads/reduce_scatter | solution.py:287
  1113.0 40.0 %reduce-scatter.23.cloned.1.call-done = bf16[128,3,256]{2,0,1:T(8,128)(2,1)} async-done(((bf16[1024,3,256]{2,0,1:T(8,128)(2,1)}), bf16[128,3,256]{2,0,1:T(8,128)(2,1)}) %reduce-scatter.23.cloned.1.call-update) | async-done | bytes 196624 | tf_op jit(solution)/shard_map/weight_grads/reduce_scatter | solution.py:287
  1154.7 77.3 %reduce-scatter.13.cloned.1.call-done = bf16[2,256,1024]{2,1,0:T(8,128)(2,1)} async-done(((bf16[2,1024,1024]{2,1,0:T(8,128)(2,1)}), bf16[2,256,1024]{2,1,0:T(8,128)(2,1)}) %reduce-scatter.13.cloned.1.call-update) | async-done | bytes 1048592 | tf_op jit(solution)/shard_map/forward/reduce_scatter | solution.py:107
  1232.0 79.5 %reduce-scatter.21.cloned.1.call-done = bf16[2,256,1024]{2,1,0:T(8,128)(2,1)} async-done(((bf16[2,1024,1024]{2,1,0:T(8,128)(2,1)}), bf16[2,256,1024]{2,1,0:T(8,128)(2,1)}) %reduce-scatter.21.cloned.1.call-update) | async-done | bytes 1048592 | tf_op jit(solution)/shard_map/backward_attention/reduce_scatter | solution.py:107
  (317 shorter events, 350.1 us)
Async XLA Ops:
  7.2 67.7 %all-reduce.3.cloned.1.call-start = ((), (), s32[]{:S(2)}) async-start(), calls=%async_computation.28 | async-start | bytes 786432
  77.0 10.2 all-to-all-start
  81.6 85.6 %all-gather.11.cloned.1.call-start = ((), (), s32[]{:S(2)}) async-start(), calls=%async_computation.12 | async-start | bytes 5242880 | tf_op jit(solution)/shard_map/forward/all_gather | solution.py:104
  89.5 121.4 %all-gather.21.cloned.1.call-start = ((), (), s32[]{:S(2)}) async-start(), calls=%async_computation.27 | async-start | bytes 3145728 | tf_op jit(solution)/shard_map/forward/all_gather | solution.py:121
  174.4 40.5 %all-gather.19.cloned.1.call-start = ((), (), s32[]{:S(2)}) async-start(), calls=%async_computation.26 | async-start | bytes 3145728 | tf_op jit(solution)/shard_map/forward/all_gather | solution.py:120
  175.0 215.6 %reduce-scatter.11.cloned.1.call-start = ((), (), s32[]{:S(2)}) async-start(), calls=%async_computation.13 | async-start | bytes 5242880 | tf_op jit(solution)/shard_map/forward/reduce_scatter | solution.py:107
  316.1 161.6 %all-gather.13.cloned.1.call-start = ((), (), s32[]{:S(2)}) async-start(), calls=%async_computation.14 | async-start | bytes 5242880 | tf_op jit(solution)/shard_map/forward/all_gather | solution.py:104
  396.3 162.2 %all-gather.15.cloned.1.call-start = ((), (), s32[]{:S(2)}) async-start(), calls=%async_computation.16 | async-start | bytes 5242880 | tf_op jit(solution)/shard_map/backward_ffn/all_gather | solution.py:104
  398.9 257.2 %reduce-scatter.15.cloned.1.call-start = ((), (), s32[]{:S(2)}) async-start(), calls=%async_computation.17 | async-start | bytes 5242880 | tf_op jit(solution)/shard_map/backward_ffn/reduce_scatter | solution.py:107
  398.9 6.7 collective-permute-start.14
  399.0 9.5 collective-permute-start.21
  405.7 6.7 collective-permute-start.15
  408.5 6.7 collective-permute-start.22
  412.4 7.5 collective-permute-start.16
  415.2 6.7 collective-permute-start.23
  419.8 6.7 collective-permute-start.17
  421.9 7.5 collective-permute-start.24
  426.5 6.7 collective-permute-start.18
  429.3 6.7 collective-permute-start.25
  433.2 6.7 collective-permute-start.19
  436.0 6.7 collective-permute-start.26
  439.9 6.7 collective-permute-start.20
  580.6 163.8 %all-gather.17.cloned.1.call-start = ((), (), s32[]{:S(2)}) async-start(), calls=%async_computation.18 | async-start | bytes 5242880 | tf_op jit(solution)/shard_map/backward_attention/all_gather | solution.py:104
  663.1 335.1 %reduce-scatter.17.cloned.1.call-start = ((), (), s32[]{:S(2)}) async-start(), calls=%async_computation.19 | async-start | bytes 3145728 | tf_op jit(solution)/shard_map/backward_attention/reduce_scatter | solution.py:243
  962.2 36.0 %reduce-scatter.19.cloned.1.call-start = ((), (), s32[]{:S(2)}) async-start(), calls=%async_computation.20 | async-start | bytes 3145728 | tf_op jit(solution)/shard_map/backward_attention/reduce_scatter | solution.py:243
  967.3 62.2 %reduce-scatter.29.cloned.1.call-start = ((), (), s32[]{:S(2)}) async-start(), calls=%async_computation.25 | async-start | bytes 2359296 | tf_op jit(solution)/shard_map/weight_grads/reduce_scatter | solution.py:287
  978.5 95.4 %reduce-scatter.27.cloned.1.call-start = ((), (), s32[]{:S(2)}) async-start(), calls=%async_computation.24 | async-start | bytes 2359296 | tf_op jit(solution)/shard_map/weight_grads/reduce_scatter | solution.py:287
  988.6 122.8 %reduce-scatter.25.cloned.1.call-start = ((), (), s32[]{:S(2)}) async-start(), calls=%async_computation.23 | async-start | bytes 589824 | tf_op jit(solution)/shard_map/weight_grads/reduce_scatter | solution.py:287
  998.1 154.9 %reduce-scatter.23.cloned.1.call-start = ((), (), s32[]{:S(2)}) async-start(), calls=%async_computation.22 | async-start | bytes 1769472 | tf_op jit(solution)/shard_map/weight_grads/reduce_scatter | solution.py:287
  1006.0 226.0 %reduce-scatter.13.cloned.1.call-start = ((), (), s32[]{:S(2)}) async-start(), calls=%async_computation.15 | async-start | bytes 5242880 | tf_op jit(solution)/shard_map/forward/reduce_scatter | solution.py:107
  1017.8 293.6 %reduce-scatter.21.cloned.1.call-start = ((), (), s32[]{:S(2)}) async-start(), calls=%async_computation.21 | async-start | bytes 5242880 | tf_op jit(solution)/shard_map/backward_attention/reduce_scatter | solution.py:107
  1325.5 10.0 all-to-all-start.1
  (62 other events, 4724.7 us)
Sparse Core Ops, SparseCore 0:
  20.4 54.5 all-reduce.2
  89.5 77.6 all-gather.10
  174.5 9.0 all-gather.20
  185.0 11.7 all-gather.18
  316.2 74.3 reduce-scatter.10
  396.4 81.2 all-gather.12
  479.2 79.2 all-gather.14
  580.7 75.2 reduce-scatter.14
  663.2 81.2 all-gather.16
  962.3 8.2 reduce-scatter.16
  972.8 11.0 reduce-scatter.18
  987.0 42.3 reduce-scatter.28
  1032.7 41.0 reduce-scatter.26
  1077.3 34.0 reduce-scatter.24
  1114.6 38.3 reduce-scatter.22
  1155.2 76.7 reduce-scatter.12
  1234.1 77.3 reduce-scatter.20
